TPU v7x, 32 devices: a whole 2x2x4 slice. The times are simulated.
32 devices in a mesh: rep: 1, dp: 32 (over x, y, z, core).
Axes of the slice: x: 2, y: 2, z: 4, core: 2. Of those that a mesh axis runs over, the one named last changes fastest.
Arguments:
- g_w_gate: bfloat16 [32, 2, 1024, 3072], P(('rep', 'dp'))
- g_w_up: bfloat16 [32, 2, 1024, 3072], P(('rep', 'dp'))
- g_w_down: bfloat16 [32, 2, 3072, 1024], P(('rep', 'dp'))
- w_gate: bfloat16 [2, 1024, 3072], replicated
- w_up: bfloat16 [2, 1024, 3072], replicated
- w_down: bfloat16 [2, 3072, 1024], replicated
- m_w_gate: float32 [2, 1024, 3072], P(None, 'dp')
- m_w_up: float32 [2, 1024, 3072], P(None, 'dp')
- m_w_down: float32 [2, 3072, 1024], P(None, 'dp')
- v_w_gate: float32 [2, 1024, 3072], P(None, 'dp')
- v_w_up: float32 [2, 1024, 3072], P(None, 'dp')
- v_w_down: float32 [2, 3072, 1024], P(None, 'dp')
Outputs:
- output 1: bfloat16 [2, 1024, 3072], P('rep')
- output 2: bfloat16 [2, 1024, 3072], P('rep')
- output 3: bfloat16 [2, 3072, 1024], P('rep')
- output 4: float32 [2, 1024, 3072], P('rep', 'dp')
- output 5: float32 [2, 1024, 3072], P('rep', 'dp')
- output 6: float32 [2, 3072, 1024], P('rep', 'dp')
- output 7: float32 [2, 1024, 3072], P('rep', 'dp')
- output 8: float32 [2, 1024, 3072], P('rep', 'dp')
- output 9: float32 [2, 3072, 1024], P('rep', 'dp')
All inputs are finite; a program needn't handle non-finite values.
Results may differ from a plain program's by a relative error of at most 0.022.
Values are sent between devices in bfloat16 or wider.
A program may use at most 2 GiB of HBM per device.

v0:
```python
import jax
import jax.numpy as jnp
from jax import lax
from jax.sharding import PartitionSpec as P


def adamw(w, m, v, g):
    m = 0.9 * m + 0.1 * g
    v = 0.95 * v + 0.05 * g * g
    step = m * lax.rsqrt(v + 1e-8) + 0.1 * w
    return (w - 0.02 * step).astype(jnp.bfloat16), m, v


def solution(mesh):
    def step(*arrays):
        terms, weights, m, v = (arrays[i : i + 3] for i in (0, 3, 6, 9))
        gradients = [lax.psum_scatter(t[0], "dp", scatter_dimension=1, tiled=True).astype(jnp.float32) for t in terms]
        me = lax.axis_index("dp")
        own = [lax.dynamic_slice_in_dim(w, me * one.shape[1], one.shape[1], 1).astype(jnp.float32) for w, one in zip(weights, m, strict=True)]
        new = [adamw(w, m, v, g) for w, m, v, g in zip(own, m, v, gradients, strict=True)]
        whole = [lax.all_gather(one[0], "dp", axis=1, tiled=True) for one in new]
        return (*whole, *(one[1] for one in new), *(one[2] for one in new))

    all_of, cut = P(None, None, None), P(None, "dp", None)
    return jax.shard_map(
        step,
        mesh=mesh,
        in_specs=(P(("rep", "dp"), None, None, None),) * 3 + (all_of,) * 3 + (cut,) * 6,
        out_specs=(P("rep", None, None),) * 3 + (P("rep", "dp", None),) * 6,
        check_vma=False,
    )
```

profile of v0, /device:TPU:0, one launch (start us, length us, event | category | flops | bytes accessed | tf_op | source)
XLA Modules:
  0.0 817.3 jit_solution(14112136312204861888)
XLA Ops:
  7.2 0.0 reduce-scatter.8.cloned.1.call-start
  7.2 0.7 reduce-scatter.8.cloned.1.call-update
  7.9 0.0 reduce-scatter.6.cloned.1.call-start
  8.0 0.0 copy-start.1
  8.0 0.0 copy-start.2
  8.0 0.0 copy-start.3
  8.0 0.0 copy-start.4
  8.0 0.7 reduce-scatter.6.cloned.1.call-update
  8.7 0.0 reduce-scatter.4.cloned.1.call-start
  8.7 0.7 reduce-scatter.4.cloned.1.call-update
  9.4 0.0 all-gather.8.cloned.1.call-start
  9.4 161.9 %reduce-scatter.8.cloned.1.call-done = bf16[2,96,1024]{2,1,0:T(8,128)(2,1)} async-done(((bf16[2,3072,1024]{2,1,0:T(8,128)(2,1)}), bf16[2,96,1024]{2,1,0:T(8,128)(2,1)}) %reduce-scatter.8.cloned.1.call-update) | async-done | bytes 393232 | tf_op jit(solution)/shard_map/reduce_scatter | solution.py:17
  171.3 0.0 copy-done.1
  171.3 2.6 fusion.10
  173.9 0.0 all-gather.8.cloned.1.call-update
  173.9 0.0 all-gather.6.cloned.1.call-start
  174.0 157.0 %reduce-scatter.6.cloned.1.call-done = bf16[2,32,3072]{2,1,0:T(8,128)(2,1)} async-done(((bf16[2,1024,3072]{2,1,0:T(8,128)(2,1)}), bf16[2,32,3072]{2,1,0:T(8,128)(2,1)}) %reduce-scatter.6.cloned.1.call-update) | async-done | bytes 393232 | tf_op jit(solution)/shard_map/reduce_scatter | solution.py:17
  330.9 0.0 copy-done.4
  330.9 2.6 fusion.6
  333.5 0.0 all-gather.6.cloned.1.call-update
  333.5 0.0 all-gather.4.cloned.1.call-start
  333.6 156.9 %reduce-scatter.4.cloned.1.call-done = bf16[2,32,3072]{2,1,0:T(8,128)(2,1)} async-done(((bf16[2,1024,3072]{2,1,0:T(8,128)(2,1)}), bf16[2,32,3072]{2,1,0:T(8,128)(2,1)}) %reduce-scatter.4.cloned.1.call-update) | async-done | bytes 393232 | tf_op jit(solution)/shard_map/reduce_scatter | solution.py:17
  490.5 3.1 fusion.2
  493.6 0.0 all-gather.4.cloned.1.call-update
  493.6 95.5 %all-gather.8.cloned.1.call-done = bf16[2,3072,1024]{2,1,0:T(8,128)(2,1)} async-done(((bf16[2,96,1024]{2,1,0:T(8,128)(2,1)}), bf16[2,3072,1024]{2,1,0:T(8,128)(2,1)}) %all-gather.8.cloned.1.call-update) | async-done | bytes 12582928 | tf_op jit(solution)/shard_map/all_gather | solution.py:21
  589.1 97.6 %all-gather.6.cloned.1.call-done = bf16[2,1024,3072]{2,1,0:T(8,128)(2,1)} async-done(((bf16[2,32,3072]{2,1,0:T(8,128)(2,1)}), bf16[2,1024,3072]{2,1,0:T(8,128)(2,1)}) %all-gather.6.cloned.1.call-update) | async-done | bytes 12582928 | tf_op jit(solution)/shard_map/all_gather | solution.py:21
  686.8 97.7 %all-gather.4.cloned.1.call-done = bf16[2,1024,3072]{2,1,0:T(8,128)(2,1)} async-done(((bf16[2,32,3072]{2,1,0:T(8,128)(2,1)}), bf16[2,1024,3072]{2,1,0:T(8,128)(2,1)}) %all-gather.4.cloned.1.call-update) | async-done | bytes 12582928 | tf_op jit(solution)/shard_map/all_gather | solution.py:21
  784.4 12.4 %copy.24 = bf16[2,1024,3072]{2,1,0:T(8,128)(2,1)} copy(bf16[2,1024,3072]{2,1,0:T(8,128)(2,1)} %all-gather.4.cloned.1.call-done) | data formatting | bytes 25165824
  796.9 6.4 copy.25
  803.3 1.1 slice-done.1
  804.3 1.3 slice-done.2
  805.6 4.8 copy.26
  (9 shorter events, 0.0 us)
Async XLA Ops:
  7.2 164.1 %reduce-scatter.8.cloned.1.call-start = ((), (), s32[]{:S(2)}) async-start(), calls=%async_computation.7 | async-start | bytes 12976128 | tf_op jit(solution)/shard_map/reduce_scatter | solution.py:17
  7.9 323.0 %reduce-scatter.6.cloned.1.call-start = ((), (), s32[]{:S(2)}) async-start(), calls=%async_computation.5 | async-start | bytes 12976128 | tf_op jit(solution)/shard_map/reduce_scatter | solution.py:17
  8.0 163.3 %copy-start.1 = (f32[2,96,1024]{2,1,0:T(8,128)S(1)}, f32[2,96,1024]{2,1,0:T(8,128)}, u32[]{:S(2)}) copy-start(f32[2,96,1024]{2,1,0:T(8,128)} %param.23) | copy-start | bytes 2359300
  8.0 163.3 %copy-start.2 = (f32[2,96,1024]{2,1,0:T(8,128)S(1)}, f32[2,96,1024]{2,1,0:T(8,128)}, u32[]{:S(2)}) copy-start(f32[2,96,1024]{2,1,0:T(8,128)} %param.20) | copy-start | bytes 2359300
  8.0 323.0 %copy-start.3 = (f32[2,32,3072]{2,1,0:T(8,128)S(1)}, f32[2,32,3072]{2,1,0:T(8,128)}, u32[]{:S(2)}) copy-start(f32[2,32,3072]{2,1,0:T(8,128)} %param.22) | copy-start | bytes 2359300
  8.0 323.0 %copy-start.4 = (f32[2,32,3072]{2,1,0:T(8,128)S(1)}, f32[2,32,3072]{2,1,0:T(8,128)}, u32[]{:S(2)}) copy-start(f32[2,32,3072]{2,1,0:T(8,128)} %param.19) | copy-start | bytes 2359300
  8.7 481.9 %reduce-scatter.4.cloned.1.call-start = ((), (), s32[]{:S(2)}) async-start(), calls=%async_computation.3 | async-start | bytes 12976128 | tf_op jit(solution)/shard_map/reduce_scatter | solution.py:17
  9.4 579.7 %all-gather.8.cloned.1.call-start = ((), (), s32[]{:S(2)}) async-start(), calls=%async_computation.8 | async-start | bytes 12976128 | tf_op jit(solution)/shard_map/all_gather | solution.py:21
  173.9 512.9 %all-gather.6.cloned.1.call-start = ((), (), s32[]{:S(2)}) async-start(), calls=%async_computation.6 | async-start | bytes 12976128 | tf_op jit(solution)/shard_map/all_gather | solution.py:21
  333.5 450.9 %all-gather.4.cloned.1.call-start = ((), (), s32[]{:S(2)}) async-start(), calls=%async_computation.4 | async-start | bytes 12976128 | tf_op jit(solution)/shard_map/all_gather | solution.py:21
  784.4 12.4 %copy-start = (bf16[2,1024,3072]{2,1,0:T(8,128)(2,1)S(1)}, bf16[2,1024,3072]{2,1,0:T(8,128)(2,1)}, u32[]{:S(2)}) copy-start(bf16[2,1024,3072]{2,1,0:T(8,128)(2,1)} %all-gather.6.cloned.1.call-done) | copy-start | bytes 37748740
  784.4 18.8 %slice-start = ((s8[12582912]{0:T(1024)(128)(4,1)}), s8[4194304]{0:T(1024)(128)(4,1)S(1)}, s32[]{:S(2)}) async-start(s8[12582912]{0:T(1024)(128)(4,1)} %bitcast.6), calls=%async_computation.9 | async-start | bytes 8388608
  784.4 19.9 %slice-start.1 = ((s8[12582912]{0:T(1024)(128)(4,1)}), s8[4194304]{0:T(1024)(128)(4,1)S(1)}, s32[]{:S(2)}) async-start(s8[12582912]{0:T(1024)(128)(4,1)} %bitcast.6), calls=%async_computation.10 | async-start | bytes 8388608
  796.9 8.8 %slice-start.2 = ((s8[12582912]{0:T(1024)(128)(4,1)}), s8[4194304]{0:T(1024)(128)(4,1)S(1)}, s32[]{:S(2)}) async-start(s8[12582912]{0:T(1024)(128)(4,1)} %bitcast.6), calls=%async_computation.11 | async-start | bytes 8388608
Sparse Core Ops, SparseCore 0:
  14.0 157.2 reduce-scatter.7
  177.3 153.5 reduce-scatter.5
  337.0 153.4 reduce-scatter.3
  494.0 95.1 all-gather.7
  592.6 94.1 all-gather.5
  690.2 94.1 all-gather.3
where the time goes:
time: 817 us
  waiting for transfers between devices  769 us (94%)
  local copies, waits for them, and re-layouts  26 us (3%)
  between operations  14.2 us (2%)
  other arithmetic  8.21 us (1%)
    reduce_scatter x3, waiting for transfers between devices, step(): lax.psum_scatter(t[0], 'dp', scatter_dimension=1, tiled=True)  476 us
    all_gather x3, waiting for transfers between devices, step(): whole = [lax.all_gather(one[0], 'dp', axis=1, tiled=True) for one in new]  291 us
    unnamed x19, local copies, waits for them, and re-layouts  26 us
  transfers between devices with their start and end apart: 6, of which 6 were waited for; matrix products, arithmetic and copies ran while one was open for 1% of the time, Pallas kernels for 0%

commit v1 on v0

v1 whole, which is shorter than its diff:
```python
import jax
import jax.numpy as jnp
from jax import lax
from jax.experimental import pallas as pl
from jax.experimental.pallas import tpu as pltpu
from jax.sharding import PartitionSpec as P

MESH = pl.DeviceIdType.MESH
STRIDE = {"x": 16, "y": 8, "h": 4, "l": 2, "c": 1}
DIMS = "xyhl"
ROWS, COLS = 32, 1024
PER_MATRIX = 6
UNITS = 18
ORDERS = ("xyhl", "yxhl", "lxyh", "xylh", "yxlh", "lyxh", "xyhl", "yxhl", "lxyh", "xylh", "yxlh", "lyxh", "xyhl", "yxhl", "lxyh", "xylh", "yxlh", "lyxh")
EVENTS = (
    0, 11, 22, 33, 44, 1, 55, 12, 66, 23, 77, 34, 88, 45, 99, 56, 110, 121, 132, 143, 154, 165, 67, 176, 78, 187, 89, 13, 2, 122,
    24, 35, 46, 57, 155, 100, 68, 111, 3, 188, 79, 90, 25, 123, 14, 58, 36, 133, 144, 47, 69, 4, 80, 112, 101, 26, 156, 91, 37,
    15, 177, 48, 124, 59, 5, 166, 70, 134, 16, 81, 113, 102, 27, 6, 145, 189, 71, 92, 82, 17, 157, 38, 178, 49, 28, 60, 167, 72,
    7, 190, 83, 18, 179, 29, 93, 39, 103, 50, 168, 114, 61, 19, 40, 125, 8, 135, 73, 30, 51, 62, 146, 84, 20, 94, 158, 21, 104, 9,
    41, 115, 10, 126, 52, 31, 74, 169, 136, 32, 180, 85, 63, 191, 147, 159, 95, 137, 105, 116, 42, 127, 43, 53, 170, 54, 64, 181,
    65, 148, 192, 75, 138, 160, 76, 86, 106, 96, 87, 117, 161, 128, 171, 149, 107, 118, 182, 193, 129, 139, 97, 98, 172, 162, 119,
    108, 120, 109, 194, 183, 140, 150, 184, 173, 130, 195, 131, 141, 142, 163, 185, 164, 151, 186, 196, 197, 174, 175, 152, 153,
)


def adamw(w, m, v, g):
    m = 0.9 * m + 0.1 * g
    v = 0.95 * v + 0.05 * g * g
    step = m * lax.rsqrt(v + 1e-8) + 0.1 * w
    return (w - 0.02 * step).astype(jnp.bfloat16), m, v


def kernel(*refs):
    g_in, w_in, m_in, v_in, w_out, m_out, v_out = (refs[i : i + 3] for i in range(0, 21, 3))
    own, rx0, rx1, rx2, rx3, rx4, w_buf, m_buf, v_buf, w_new, rs_send, rs_recv, ag_send, ag_recv, local = refs[21:]
    rx = (rx0, rx1, rx2, rx3, rx4)
    me = lax.axis_index("dp")
    bit = {d: (me // s) % 2 for d, s in STRIDE.items()}
    partner = {d: me + (1 - 2 * bit[d]) * s for d, s in STRIDE.items()}
    every = slice(None)

    barrier = pltpu.get_barrier_semaphore()
    for d in STRIDE:
        pl.semaphore_signal(barrier, inc=1, device_id=(0, partner[d]), device_id_type=MESH)
    pl.semaphore_wait(barrier, len(STRIDE))

    def place(u):
        which, rest = divmod(u, PER_MATRIX)
        layer, part = divmod(rest, PER_MATRIX // 2)
        if which < 2:
            return which, layer, (every, pl.ds(part * COLS, COLS))
        return which, layer, (pl.ds(part * ROWS, ROWS), every)

    def blocks(ref, u, at, core):
        _, layer, within = place(u)
        return ref.at[(layer, *(at.get(d, every) for d in DIMS), core, *within)]

    def mine(ref, u):
        _, layer, within = place(u)
        return ref.at[(layer, *within)]

    def fixed(u, k, flip):
        at = {d: bit[d] for d in ORDERS[u][:k]}
        if flip:
            at[ORDERS[u][k - 1]] = 1 - bit[ORDERS[u][k - 1]]
        return at

    def remote(src, dst, send, recv, d):
        return pltpu.make_async_remote_copy(
            src_ref=src, dst_ref=dst, send_sem=send, recv_sem=recv, device_id=(0, partner[d]), device_id_type=MESH
        )

    def scatter(u, k):
        if k == 0:
            src, d = blocks(g_in[place(u)[0]], u, {}, 1 - bit["c"]), "c"
        else:
            at, d = fixed(u, k, True), ORDERS[u][k - 1]
            src = own.at[(u, *(at.get(d, every) for d in DIMS))]
        return remote(src, rx[k].at[u], rs_send.at[u, k], rs_recv.at[u, k], d)

    def gather(u, k, receive=False):
        ref, at, core = w_out[place(u)[0]], fixed(u, k, receive and k > 0), bit["c"]
        if k == 0 and receive:
            core = 1 - core
        dst = blocks(ref, u, at, core)
        src = w_new.at[u] if k == 4 else dst
        return remote(src, dst, ag_send.at[u, k], ag_recv.at[u, k], ORDERS[u][k - 1] if k else "c")

    def copy(src, dst, u, i):
        return pltpu.make_async_copy(src, dst, local.at[u, i])

    def load_own(u):
        return copy(blocks(g_in[place(u)[0]], u, {}, bit["c"]), own.at[u], u, 0)

    def loads(u):
        which = place(u)[0]
        return (
            copy(blocks(w_in[which], u, bit, bit["c"]), w_buf.at[u], u, 1),
            copy(mine(m_in[which], u), m_buf.at[u], u, 2),
            copy(mine(v_in[which], u), v_buf.at[u], u, 3),
        )

    def stores(u):
        which = place(u)[0]
        return (
            copy(w_new.at[u], blocks(w_out[which], u, bit, bit["c"]), u, 4),
            copy(m_buf.at[u], mine(m_out[which], u), u, 5),
            copy(v_buf.at[u], mine(v_out[which], u), u, 6),
        )

    def total(u, at, steps, rows):
        so_far = own[(u, *(at[d] for d in DIMS), rows)].astype(jnp.float32)
        for j in range(steps):
            left = [d for d in DIMS if d not in ORDERS[u][:j]]
            so_far += rx[j][(u, *(at[d] for d in left), rows)].astype(jnp.float32)
        return so_far

    def reduce_to_send(u, k):
        base = fixed(u, k, True)
        free = [d for d in DIMS if d not in base]

        def body(i, carry):
            at = dict(base)
            for p, d in enumerate(reversed(free)):
                at[d] = (i // 2**p) % 2
            for half in range(2):
                rows = pl.ds(half * (ROWS // 2), ROWS // 2)
                own[(u, *(at[d] for d in DIMS), rows)] = total(u, at, k, rows).astype(jnp.bfloat16)
            return carry

        lax.fori_loop(0, 2 ** len(free), body, 0)

    def update(u):
        for half in range(2):
            rows = pl.ds(half * (ROWS // 2), ROWS // 2)
            g = total(u, bit, 5, rows).astype(jnp.bfloat16).astype(jnp.float32)
            w_new[u, rows], m_buf[u, rows], v_buf[u, rows] = adamw(w_buf[u, rows].astype(jnp.float32), m_buf[u, rows], v_buf[u, rows], g)

    def event(u, e):
        if e == 0:
            scatter(u, 0).start()
            load_own(u).start()
        elif e <= 4:
            if e == 1:
                load_own(u).wait()
                for one in loads(u):
                    one.start()
            scatter(u, e - 1).wait_recv()
            reduce_to_send(u, e)
            scatter(u, e).start()
        elif e == 5:
            for one in loads(u):
                one.wait()
            scatter(u, 4).wait_recv()
            update(u)
            gather(u, 4).start()
            for one in stores(u):
                one.start()
        elif e <= 9:
            if e == 6:
                for one in stores(u):
                    one.wait()
            gather(u, 10 - e, receive=True).wait_recv()
            gather(u, 9 - e).start()
        else:
            gather(u, 0, receive=True).wait_recv()

    for code in EVENTS:
        event(*divmod(code, 11))
    for u in range(UNITS):
        for k in range(5):
            scatter(u, k).wait_send()
            gather(u, k).wait_send()


def solution(mesh):
    def step(*arrays):
        split = [(2, 2, 2, 2, 2, 2, a.shape[-2] // 32, a.shape[-1]) for a in arrays[:3]]
        terms = [a.reshape(s) for a, s in zip(arrays[:3], split)]
        weights = [a.reshape(s) for a, s in zip(arrays[3:6], split)]
        block = (UNITS, ROWS, COLS)
        dma = pltpu.SemaphoreType.DMA
        anywhere = pl.BlockSpec(memory_space=pl.ANY)
        out = pl.pallas_call(
            kernel,
            out_shape=[jax.ShapeDtypeStruct(s, jnp.bfloat16) for s in split] + [jax.ShapeDtypeStruct(a.shape, a.dtype) for a in arrays[6:]],
            in_specs=[anywhere] * 12,
            out_specs=[anywhere] * 9,
            scratch_shapes=[
                pltpu.VMEM((UNITS, 2, 2, 2, 2, ROWS, COLS), jnp.bfloat16),
                pltpu.VMEM((UNITS, 2, 2, 2, 2, ROWS, COLS), jnp.bfloat16),
                pltpu.VMEM((UNITS, 2, 2, 2, ROWS, COLS), jnp.bfloat16),
                pltpu.VMEM((UNITS, 2, 2, ROWS, COLS), jnp.bfloat16),
                pltpu.VMEM((UNITS, 2, ROWS, COLS), jnp.bfloat16),
                pltpu.VMEM(block, jnp.bfloat16),
                pltpu.VMEM(block, jnp.bfloat16),
                pltpu.VMEM(block, jnp.float32),
                pltpu.VMEM(block, jnp.float32),
                pltpu.VMEM(block, jnp.bfloat16),
                dma((UNITS, 5)),
                dma((UNITS, 5)),
                dma((UNITS, 5)),
                dma((UNITS, 5)),
                dma((UNITS, 7)),
            ],
            compiler_params=pltpu.CompilerParams(collective_id=0, has_side_effects=True, vmem_limit_bytes=67_043_328),
            name="zero_step",
        )(*terms, *weights, *arrays[6:])
        return (*(o.reshape(a.shape) for o, a in zip(out[:3], arrays[3:6])), *out[3:])

    all_of, cut = P(None, None, None), P(None, "dp", None)
    return jax.shard_map(
        step,
        mesh=mesh,
        in_specs=(P(("rep", "dp"), None, None, None),) * 3 + (all_of,) * 3 + (cut,) * 6,
        out_specs=(P("rep", None, None),) * 3 + (P("rep", "dp", None),) * 6,
        check_vma=False,
    )
```

time: 817 us -> 322 us (0.39)
  waiting for transfers between devices: 769 us -> 0 us
  Pallas kernels: 0 us -> 288 us
  between operations: 14.2 us -> 0.71 us
  other arithmetic: 8.21 us -> 0.01 us
    reduce_scatter x3 -> x0, waiting for transfers between devices: 476 us -> none  [step(): lax.psum_scatter(t[0], 'dp', scatter_dimension=1, tiled=True)]
    all_gather x3 -> x0, waiting for transfers between devices: 291 us -> none  [step(): whole = [lax.all_gather(one[0], 'dp', axis=1, tiled=True) for one in new]]
    pallas_call x0 -> x1, Pallas kernels: none -> 288 us  [step(): pl.pallas_call(kernel, out_shape=[jax.ShapeDtypeStruct(s, jnp.bfloat16) f...]
    convert_element_type x3 -> x0, other arithmetic: 8.21 us -> none  [adamw(): return ((w - 0.02 * step).astype(jnp.bfloat16), m, v)]
    unnamed x19 -> x29, local copies, waits for them, and re-layouts: 26 us -> 32.3 us
  transfers between devices with their start and end apart: 6 -> 0, of which waited for: 6 -> 0; matrix products, arithmetic and copies ran while one was open for 1% -> 0% of each run, Pallas kernels for 0% -> 0%
where the time goes in v1:
time: 322 us; the launch traced here: 321 us
  Pallas kernels  288 us (89%)
  local copies, waits for them, and re-layouts  32.3 us (10%)
    pallas_call x1, Pallas kernels, step(): pl.pallas_call(kernel, out_shape=[jax.ShapeDtypeStruct(s, jnp.bfloat16) f...  288 us
    unnamed x29, local copies, waits for them, and re-layouts  32.3 us

profile of v1, /device:TPU:0, one launch (start us, length us, event | category | flops | bytes accessed | tf_op | source)
XLA Modules:
  0.0 320.7 jit_solution(12461023136653703106)
XLA Ops:
  0.6 287.7 %zero_step.1 = (bf16[2,2,2,2,2,2,32,3072]{7,6,5,4,3,2,1,0:T(8,128)(2,1)}, bf16[2,2,2,2,2,2,32,3072]{7,6,5,4,3,2,1,0:T(8,128)(2,1)}, bf16[2,2,2,2,2,2,96,1024]{7,...) custom-call(bf16[2,2,2,2,2,2,32,3072]{7,6,5,4,3,2,1,0:T(8,128)(2,1)}, ...), custom_call_target="tpu_custom_call" | custom-call | tf_op jit(solution)/shard_map/zero_step/pallas_call | solution.py:184
  288.4 0.0 copy-start
  288.4 0.0 slice-start
  288.4 0.0 slice-start.1
  288.4 12.4 %copy.30 = bf16[2,1024,3072]{2,1,0:T(8,128)(2,1)} copy(bf16[2,1024,3072]{2,1,0:T(8,128)(2,1)} %bitcast.19) | data formatting | bytes 25165824
  300.8 0.0 copy-done
  300.8 0.0 slice-start.2
  300.8 6.4 %copy.31 = bf16[2,1024,3072]{2,1,0:T(8,128)(2,1)} copy(bf16[2,1024,3072]{2,1,0:T(8,128)(2,1)S(1)} %bitcast.18) | data formatting | bytes 25165824
  307.2 0.0 slice-done
  307.2 1.0 slice-done.1
  308.3 1.3 slice-done.2
  309.6 0.0 copy-start.6
  309.6 0.0 copy-start.5
  309.6 0.0 copy-start.4
  309.6 0.0 copy-start.3
  309.6 0.0 copy-start.2
  309.6 0.0 copy-start.1
  309.6 5.8 %copy.32 = bf16[2,3072,1024]{2,1,0:T(8,128)(2,1)} copy(bf16[2,3072,1024]{2,1,0:T(8,128)(2,1)S(1)} %bitcast.17) | data formatting | bytes 25165824
  315.4 0.0 copy-done.6
  315.4 0.9 copy.33
  316.3 0.0 copy-done.5
  316.3 0.9 copy.34
  317.2 0.0 copy-done.4
  317.2 0.9 copy.35
  318.1 0.0 copy-done.3
  318.1 0.9 copy.36
  319.0 0.0 copy-done.2
  319.0 0.9 copy.37
  319.9 0.0 copy-done.1
  319.9 0.9 copy.38
  (1 shorter events, 0.0 us)
Async XLA Ops:
  288.4 12.5 %copy-start = (bf16[2,2,2,2,2,2,32,3072]{7,6,5,4,3,2,1,0:T(8,128)(2,1)S(1)}, bf16[2,2,2,2,2,2,32,3072]{7,6,5,4,3,2,1,0:T(8,128)(2,1)}, u32[]{:S(2)}) copy-start(bf16[2,2,2,2,2,2,32,3072]{7,6,5,4,3,2,1,0:T(8,128)(2,1)} %get-tuple-element.19) | copy-start | bytes 37748740
  288.4 18.8 %slice-start = ((s8[12582912]{0:T(1024)(128)(4,1)}), s8[4194304]{0:T(1024)(128)(4,1)S(1)}, s32[]{:S(2)}) async-start(s8[12582912]{0:T(1024)(128)(4,1)} %bitcast.15), calls=%async_computation | async-start | bytes 8388608
  288.4 19.9 %slice-start.1 = ((s8[12582912]{0:T(1024)(128)(4,1)}), s8[4194304]{0:T(1024)(128)(4,1)S(1)}, s32[]{:S(2)}) async-start(s8[12582912]{0:T(1024)(128)(4,1)} %bitcast.15), calls=%async_computation.1 | async-start | bytes 8388608
  300.8 8.7 %slice-start.2 = ((s8[12582912]{0:T(1024)(128)(4,1)}), s8[4194304]{0:T(1024)(128)(4,1)S(1)}, s32[]{:S(2)}) async-start(s8[12582912]{0:T(1024)(128)(4,1)} %bitcast.15), calls=%async_computation.2 | async-start | bytes 8388608
  309.6 5.9 %copy-start.6 = (f32[2,32,3072]{2,1,0:T(8,128)S(1)}, f32[2,32,3072]{2,1,0:T(8,128)}, u32[]{:S(2)}) copy-start(f32[2,32,3072]{2,1,0:T(8,128)} %get-tuple-element.39) | copy-start | bytes 2359300
  309.6 6.7 %copy-start.5 = (f32[2,32,3072]{2,1,0:T(8,128)S(1)}, f32[2,32,3072]{2,1,0:T(8,128)}, u32[]{:S(2)}) copy-start(f32[2,32,3072]{2,1,0:T(8,128)} %get-tuple-element.40) | copy-start | bytes 2359300
  309.6 7.6 %copy-start.4 = (f32[2,96,1024]{2,1,0:T(8,128)S(1)}, f32[2,96,1024]{2,1,0:T(8,128)}, u32[]{:S(2)}) copy-start(f32[2,96,1024]{2,1,0:T(8,128)} %get-tuple-element.41) | copy-start | bytes 2359300
  309.6 8.5 %copy-start.3 = (f32[2,32,3072]{2,1,0:T(8,128)S(1)}, f32[2,32,3072]{2,1,0:T(8,128)}, u32[]{:S(2)}) copy-start(f32[2,32,3072]{2,1,0:T(8,128)} %get-tuple-element.42) | copy-start | bytes 2359300
  309.6 9.4 %copy-start.2 = (f32[2,32,3072]{2,1,0:T(8,128)S(1)}, f32[2,32,3072]{2,1,0:T(8,128)}, u32[]{:S(2)}) copy-start(f32[2,32,3072]{2,1,0:T(8,128)} %get-tuple-element.43) | copy-start | bytes 2359300
  309.6 10.3 %copy-start.1 = (f32[2,96,1024]{2,1,0:T(8,128)S(1)}, f32[2,96,1024]{2,1,0:T(8,128)}, u32[]{:S(2)}) copy-start(f32[2,96,1024]{2,1,0:T(8,128)} %get-tuple-element.44) | copy-start | bytes 2359300

commit v2 on v1

v2 whole, which is shorter than its diff:
```python
import jax
import jax.numpy as jnp
from jax import lax
from jax.experimental import pallas as pl
from jax.experimental.pallas import tpu as pltpu
from jax.sharding import PartitionSpec as P

MESH = pl.DeviceIdType.MESH
STRIDE = {"x": 16, "y": 8, "h": 4, "l": 2, "c": 1}
DIMS = "xyhl"
ROWS, COLS = 32, 1024
PER_MATRIX = 6
UNITS = 18
KERNEL_VMEM = int(18.25 * 2**20)
GROUP = 3
RING = 3
ORDERS = ("yxhl", "lxyh", "yxlh", "xylh", "lyxh", "xyhl", "yxlh", "lyxh", "xylh", "xyhl", "lyxh", "lxyh", "yxlh", "xyhl", "yxlh", "lxyh", "xylh", "yxlh")
EVENTS = (
    0, 11, 33, 22, 55, 66, 99, 88, 44, 77, 143, 121, 132, 110, 154, 176, 165, 187, 1, 12, 34, 23, 56, 45, 67, 78, 100, 35, 122, 2,
    133, 13, 111, 24, 57, 68, 101, 36, 89, 3, 46, 166, 14, 123, 79, 25, 134, 112, 58, 69, 144, 155, 37, 4, 102, 15, 47, 90, 26,
    80, 167, 135, 124, 70, 59, 188, 5, 177, 38, 103, 136, 16, 48, 145, 60, 156, 27, 81, 91, 6, 104, 113, 39, 168, 71, 61, 17, 189,
    92, 28, 178, 49, 105, 40, 157, 7, 18, 125, 72, 82, 29, 190, 179, 114, 62, 137, 8, 41, 93, 146, 50, 19, 73, 106, 30, 126, 63,
    158, 9, 180, 138, 10, 169, 94, 42, 115, 43, 83, 51, 191, 107, 147, 20, 74, 21, 127, 31, 159, 32, 139, 181, 52, 95, 170, 64,
    65, 116, 84, 148, 192, 160, 75, 182, 76, 128, 108, 109, 53, 96, 54, 140, 149, 171, 117, 85, 193, 161, 183, 129, 150, 141, 142,
    172, 97, 98, 86, 118, 87, 194, 162, 184, 173, 151, 130, 195, 131, 163, 119, 185, 164, 120, 186, 196, 174, 152, 197, 175, 153,
)
TURN = {code // 11: i for i, code in enumerate(c for c in EVENTS if c % 11 == 5)}


def adamw(w, m, v, g):
    m = 0.9 * m + 0.1 * g
    v = 0.95 * v + 0.05 * g * g
    step = m * lax.rsqrt(v + 1e-8) + 0.1 * w
    return (w - 0.02 * step).astype(jnp.bfloat16), m, v


def place(u):
    which, rest = divmod(u, PER_MATRIX)
    layer, part = divmod(rest, PER_MATRIX // 2)
    if which < 2:
        return which, layer, (slice(None), pl.ds(part * COLS, COLS))
    return which, layer, (pl.ds(part * ROWS, ROWS), slice(None))


def blocks(ref, u, at, core):
    _, layer, within = place(u)
    return ref.at[(layer, *(at.get(d, slice(None)) for d in DIMS), core, *within)]


def mine(ref, u):
    _, layer, within = place(u)
    return ref.at[(layer, *within)]


def kernel(*refs):
    g_in, w_in, m_in, v_in = (refs[i : i + 3] for i in range(0, 12, 3))
    n = UNITS // GROUP
    own = [one.at[i] for one in refs[12 : 12 + n] for i in range(GROUP)]
    rx0 = [one.at[i] for one in refs[12 + n : 12 + 2 * n] for i in range(GROUP)]
    g_buf, rx1, rx2, rx3, rx4, w_buf, m_buf, v_buf, rs_send, rs_recv, ag_send, ag_recv, local, free = refs[12 + 2 * n :]
    rx = (rx0, *([one.at[u] for u in range(UNITS)] for one in (rx1, rx2, rx3, rx4)))
    me = lax.axis_index("dp")
    bit = {d: (me // s) % 2 for d, s in STRIDE.items()}
    partner = {d: me + (1 - 2 * bit[d]) * s for d, s in STRIDE.items()}
    every = slice(None)

    barrier = pltpu.get_barrier_semaphore()
    for d in STRIDE:
        pl.semaphore_signal(barrier, inc=1, device_id=(0, partner[d]), device_id_type=MESH)
    pl.semaphore_wait(barrier, len(STRIDE))

    def fixed(u, k, flip):
        at = {d: bit[d] for d in ORDERS[u][:k]}
        if flip:
            at[ORDERS[u][k - 1]] = 1 - bit[ORDERS[u][k - 1]]
        return at

    def remote(src, dst, send, recv, d):
        return pltpu.make_async_remote_copy(
            src_ref=src, dst_ref=dst, send_sem=send, recv_sem=recv, device_id=(0, partner[d]), device_id_type=MESH
        )

    def scatter(u, k):
        if k == 0:
            src, d = blocks(g_in[place(u)[0]], u, {}, 1 - bit["c"]), "c"
        else:
            at, d = fixed(u, k, True), ORDERS[u][k - 1]
            src = own[u].at[tuple(at.get(d, every) for d in DIMS)]
        return remote(src, rx[k][u], rs_send.at[u, k], rs_recv.at[u, k], d)

    def gather(u, k, receive=False):
        if k == 0:
            return remote(own[u], rx0[u], ag_send.at[u, 0], ag_recv.at[u, 0], "c")
        at = fixed(u, k, receive)
        region = own[u].at[tuple(at.get(d, every) for d in DIMS)]
        return remote(region, region, ag_send.at[u, k], ag_recv.at[u, k], ORDERS[u][k - 1])

    def copy(src, dst, u, i):
        return pltpu.make_async_copy(src, dst, local.at[u, i])

    def load_own(u):
        return copy(blocks(g_in[place(u)[0]], u, {}, bit["c"]), own[u], u, 0)

    def loads(u):
        which, slot = place(u)[0], TURN[u] % RING
        return (
            copy(blocks(w_in[which], u, bit, bit["c"]), w_buf.at[slot], u, 1),
            copy(mine(m_in[which], u), m_buf.at[slot], u, 2),
            copy(mine(v_in[which], u), v_buf.at[slot], u, 3),
        )

    def total(u, at, steps, rows):
        so_far = own[u][(*(at[d] for d in DIMS), rows)].astype(jnp.float32)
        for j in range(steps):
            left = [d for d in DIMS if d not in ORDERS[u][:j]]
            so_far += rx[j][u][(*(at[d] for d in left), rows)].astype(jnp.float32)
        return so_far

    def reduce_to_send(u, k):
        base = fixed(u, k, True)
        free = [d for d in DIMS if d not in base]

        def body(i, carry):
            at = dict(base)
            for p, d in enumerate(reversed(free)):
                at[d] = (i // 2**p) % 2
            for half in range(2):
                rows = pl.ds(half * (ROWS // 2), ROWS // 2)
                own[u][(*(at[d] for d in DIMS), rows)] = total(u, at, k, rows).astype(jnp.bfloat16)
            return carry

        lax.fori_loop(0, 2 ** len(free), body, 0)

    def update(u):
        slot = TURN[u] % RING
        for half in range(2):
            rows = pl.ds(half * (ROWS // 2), ROWS // 2)
            g = total(u, bit, 5, rows).astype(jnp.bfloat16)
            g_buf[u, rows] = g
            w, m, v = w_buf[slot, rows].astype(jnp.float32), m_buf[slot, rows], v_buf[slot, rows]
            own[u][(*(bit[d] for d in DIMS), rows)] = adamw(w, m, v, g.astype(jnp.float32))[0]

    def release(u, k):
        pl.semaphore_signal(free.at[u, k], inc=1, device_id=(0, partner[ORDERS[u][k - 1] if k else "c"]), device_id_type=MESH)

    def arrived(u, k):
        scatter(u, k).wait_recv()
        if k:
            scatter(u, k).wait_send()
            release(u, k)

    def send_back(u, k):
        pl.semaphore_wait(free.at[u, k], 1)
        gather(u, k).start()

    def event(u, e):
        if e == 0:
            scatter(u, 0).start()
            load_own(u).start()
        elif e <= 4:
            if e == 1:
                load_own(u).wait()
            arrived(u, e - 1)
            reduce_to_send(u, e)
            scatter(u, e).start()
        elif e == 5:
            for one in loads(u):
                one.wait()
            arrived(u, 4)
            update(u)
            for next_u, turn in TURN.items():
                if turn == TURN[u] + RING:
                    for one in loads(next_u):
                        one.start()
            release(u, 0)
            send_back(u, 4)
        elif e <= 9:
            gather(u, 10 - e, receive=True).wait_recv()
            send_back(u, 9 - e)
        else:
            gather(u, 0, receive=True).wait_recv()

    for u, turn in TURN.items():
        if turn < RING:
            for one in loads(u):
                one.start()
    for code in EVENTS:
        event(*divmod(code, 11))
    for u in range(UNITS):
        scatter(u, 0).wait_send()
        for k in range(5):
            gather(u, k).wait_send()


def write_out(*refs):
    n = UNITS // GROUP
    own, rx0, g_buf = refs[:n], refs[n : 2 * n], refs[2 * n]
    m_in, v_in, w_out, m_out, v_out = (refs[2 * n + i : 2 * n + i + 3] for i in (1, 4, 7, 10, 13))
    m_buf, v_buf, sems = refs[2 * n + 16 :]
    core = lax.axis_index("dp") % 2

    def copy(src, dst, u, i):
        return pltpu.make_async_copy(src, dst, sems.at[u, i])

    def loads(u):
        which = place(u)[0]
        return copy(mine(m_in[which], u), m_buf.at[u], u, 0), copy(mine(v_in[which], u), v_buf.at[u], u, 1)

    def stores(u):
        which = place(u)[0]
        return copy(m_buf.at[u], mine(m_out[which], u), u, 2), copy(v_buf.at[u], mine(v_out[which], u), u, 3)

    def weights(u):
        which = place(u)[0]
        return (
            copy(own[u // GROUP].at[u % GROUP], blocks(w_out[which], u, {}, core), u, 4),
            copy(rx0[u // GROUP].at[u % GROUP], blocks(w_out[which], u, {}, 1 - core), u, 5),
        )

    for u in reversed(range(UNITS)):
        for one in reversed(weights(u)):
            one.start()
    for u in range(UNITS):
        for one in loads(u):
            one.start()
    for u in range(UNITS):
        for one in loads(u):
            one.wait()
        for half in range(2):
            rows = pl.ds(half * (ROWS // 2), ROWS // 2)
            g = g_buf[u, rows].astype(jnp.float32)
            _, m_buf[u, rows], v_buf[u, rows] = adamw(g, m_buf[u, rows], v_buf[u, rows], g)
        for one in stores(u):
            one.start()
    for u in range(UNITS):
        for one in (*weights(u), *stores(u)):
            one.wait()


def solution(mesh):
    def step(*arrays):
        split = [(2, 2, 2, 2, 2, 2, a.shape[-2] // 32, a.shape[-1]) for a in arrays[:3]]
        terms = [a.reshape(s) for a, s in zip(arrays[:3], split)]
        weights = [a.reshape(s) for a, s in zip(arrays[3:6], split)]
        block = (UNITS, ROWS, COLS)
        dma = pltpu.SemaphoreType.DMA
        anywhere = pl.BlockSpec(memory_space=pltpu.HBM)
        vmem = pl.BlockSpec(memory_space=pltpu.VMEM)
        half = pltpu.VMEM((GROUP, 2, 2, 2, 2, ROWS, COLS), jnp.bfloat16)
        kept = pl.pallas_call(
            kernel,
            out_shape=[half] * (2 * UNITS // GROUP) + [pltpu.VMEM(block, jnp.bfloat16)],
            in_specs=[anywhere] * 12,
            out_specs=[vmem] * (2 * UNITS // GROUP + 1),
            scratch_shapes=[
                pltpu.VMEM((UNITS, 2, 2, 2, ROWS, COLS), jnp.bfloat16),
                pltpu.VMEM((UNITS, 2, 2, ROWS, COLS), jnp.bfloat16),
                pltpu.VMEM((UNITS, 2, ROWS, COLS), jnp.bfloat16),
                pltpu.VMEM(block, jnp.bfloat16),
                pltpu.VMEM((RING, ROWS, COLS), jnp.bfloat16),
                pltpu.VMEM((RING, ROWS, COLS), jnp.float32),
                pltpu.VMEM((RING, ROWS, COLS), jnp.float32),
                dma((UNITS, 5)),
                dma((UNITS, 5)),
                dma((UNITS, 5)),
                dma((UNITS, 5)),
                dma((UNITS, 4)),
                pltpu.SemaphoreType.REGULAR((UNITS, 5)),
            ],
            compiler_params=pltpu.CompilerParams(collective_id=0, has_side_effects=True, vmem_limit_bytes=KERNEL_VMEM),
            name="zero_step",
        )(*terms, *weights, *arrays[6:])
        out = pl.pallas_call(
            write_out,
            out_shape=[jax.ShapeDtypeStruct(s, jnp.bfloat16) for s in split] + [jax.ShapeDtypeStruct(a.shape, a.dtype) for a in arrays[6:]],
            in_specs=[vmem] * (2 * UNITS // GROUP + 1) + [anywhere] * 6,
            out_specs=[anywhere] * 9,
            scratch_shapes=[pltpu.VMEM(block, jnp.float32), pltpu.VMEM(block, jnp.float32), dma((UNITS, 6))],
            compiler_params=pltpu.CompilerParams(vmem_limit_bytes=KERNEL_VMEM),
            name="write_out",
        )(*kept, *(pltpu.with_memory_space_constraint(a, pltpu.HBM) for a in arrays[6:]))
        return (*(o.reshape(a.shape) for o, a in zip(out[:3], arrays[3:6])), *out[3:])

    all_of, cut = P(None, None, None), P(None, "dp", None)
    return jax.shard_map(
        step,
        mesh=mesh,
        in_specs=(P(("rep", "dp"), None, None, None),) * 3 + (all_of,) * 3 + (cut,) * 6,
        out_specs=(P("rep", None, None),) * 3 + (P("rep", "dp", None),) * 6,
        check_vma=False,
    )
```

time: 322 us -> 296 us (0.919)
  local copies, waits for them, and re-layouts: 32.3 us -> 1.64 us
  Pallas kernels: 288 us -> 294 us
    unnamed x29 -> x2, local copies, waits for them, and re-layouts: 32.3 us -> 1.64 us
    pallas_call x1 -> x2, Pallas kernels: 288 us -> 294 us  [the longest x1 276 us: step(): pl.pallas_call(kernel, out_shape=[half] * (2 * UNITS // GROUP) + [pltpu.V...]
where the time goes in v2:
time: 296 us
  Pallas kernels  294 us (99%)
    pallas_call x1, Pallas kernels, step(): pl.pallas_call(kernel, out_shape=[half] * (2 * UNITS // GROUP) + [pltpu.V...  276 us
    pallas_call x1, Pallas kernels, step(): pl.pallas_call(write_out, out_shape=[jax.ShapeDtypeStruct(s, jnp.bfloat16...  17.6 us

profile of v2, /device:TPU:0, one launch (start us, length us, event | category | flops | bytes accessed | tf_op | source)
XLA Modules:
  0.0 296.1 jit_solution(4580416200377952362)
XLA Ops:
  0.6 276.2 %zero_step.1 = (bf16[3,2,2,2,2,32,1024]{6,5,4,3,2,1,0:T(8,128)(2,1)S(1)}, bf16[3,2,2,2,2,32,1024]{6,5,4,3,2,1,0:T(8,128)(2,1)S(1)}, bf16[3,2,2,2,2,32,1024]{6,5,...) custom-call(bf16[2,2,2,2,2,2,32,3072]{7,6,5,4,3,2,1,0:T(8,128)(2,1)}, ...), custom_call_target="tpu_custom_call" | custom-call | tf_op jit(solution)/shard_map/zero_step/pallas_call | solution.py:250
  276.8 0.0 copy-start
  276.8 1.6 copy-done
  278.5 17.6 %write_out.1 = (bf16[2,2,2,2,2,2,32,3072]{7,6,5,4,3,2,1,0:T(8,128)(2,1)}, bf16[2,2,2,2,2,2,32,3072]{7,6,5,4,3,2,1,0:T(8,128)(2,1)}, bf16[2,2,2,2,2,2,96,1024]{7,...) custom-call(bf16[3,2,2,2,2,32,1024]{6,5,4,3,2,1,0:T(8,128)(2,1)S(1)}, ...), custom_call_target="tpu_custom_call" | custom-call | tf_op jit(solution)/shard_map/write_out/pallas_call | solution.py:273
Async XLA Ops:
  276.8 1.7 copy-start

commit v3 on v2

v3 whole, which is shorter than its diff:
```python
import jax
import jax.numpy as jnp
from jax import lax
from jax.experimental import pallas as pl
from jax.experimental.pallas import tpu as pltpu
from jax.sharding import PartitionSpec as P

MESH = pl.DeviceIdType.MESH
STRIDE = {"x": 16, "y": 8, "h": 4, "l": 2, "c": 1}
DIMS = "xyhl"
ROWS, COLS = 32, 1024
PER_MATRIX = 6
UNITS = 18
KERNEL_VMEM = int(10.75 * 2**20)
GROUP = 6
ORDERS = ("yxhl", "lxyh", "lyxh", "xylh", "xylh", "xylh", "yxlh", "xylh", "lxyh", "lyxh", "lyxh", "yxlh", "xylh", "yxlh", "yxlh", "yxlh", "lxyh", "xylh")
EVENTS = (
    22, 66, 33, 44, 99, 55, 110, 0, 77, 121, 11, 143, 154, 165, 132, 23, 88, 67, 187, 34, 176, 45, 100, 56, 111, 1, 122, 12, 144,
    78, 89, 24, 68, 35, 2, 177, 46, 133, 101, 57, 123, 112, 13, 69, 79, 25, 36, 3, 145, 155, 47, 90, 102, 70, 134, 188, 37, 58,
    124, 166, 48, 4, 71, 26, 113, 59, 38, 80, 178, 125, 146, 14, 5, 49, 72, 91, 27, 156, 103, 81, 60, 39, 135, 147, 6, 126, 50,
    73, 189, 114, 28, 167, 104, 15, 40, 179, 82, 92, 61, 136, 157, 148, 190, 51, 74, 7, 41, 29, 127, 180, 115, 168, 105, 62, 52,
    16, 158, 8, 83, 93, 191, 137, 128, 75, 149, 42, 76, 181, 169, 30, 106, 116, 43, 17, 84, 63, 159, 94, 150, 53, 192, 138, 54, 9,
    129, 117, 10, 170, 107, 18, 31, 182, 160, 32, 85, 139, 64, 193, 95, 171, 65, 151, 19, 108, 130, 161, 109, 131, 194, 118, 172,
    183, 86, 87, 140, 96, 20, 162, 21, 152, 173, 153, 119, 195, 184, 120, 97, 163, 141, 98, 164, 142, 185, 174, 196, 186, 175, 197,
)


def adamw(w, m, v, g):
    m = 0.9 * m + 0.1 * g
    v = 0.95 * v + 0.05 * g * g
    step = m * lax.rsqrt(v + 1e-8) + 0.1 * w
    return (w - 0.02 * step).astype(jnp.bfloat16), m, v


def place(u):
    which, rest = divmod(u, PER_MATRIX)
    layer, part = divmod(rest, PER_MATRIX // 2)
    if which < 2:
        return which, layer, (slice(None), pl.ds(part * COLS, COLS))
    return which, layer, (pl.ds(part * ROWS, ROWS), slice(None))


def blocks(ref, u, at, core):
    _, layer, within = place(u)
    return ref.at[(layer, *(at.get(d, slice(None)) for d in DIMS), core, *within)]


def mine(ref, u):
    _, layer, within = place(u)
    return ref.at[(layer, *within)]


def kernel(*refs):
    g_in, w_in, m_in, v_in = (refs[i : i + 3] for i in range(0, 12, 3))
    n = UNITS // GROUP
    own = [one.at[i] for one in refs[12 : 12 + n] for i in range(GROUP)]
    rx0 = [one.at[i] for one in refs[12 + n : 12 + 2 * n] for i in range(GROUP)]
    m_buf, v_buf, rx1, w_buf, rs_send, rs_recv, ag_send, ag_recv, local, free, ready = refs[12 + 2 * n :]
    me = lax.axis_index("dp")
    bit = {d: (me // s) % 2 for d, s in STRIDE.items()}
    partner = {d: me + (1 - 2 * bit[d]) * s for d, s in STRIDE.items()}
    every = slice(None)

    def later(u, k):
        first = ORDERS[u][0]
        rest = [d for d in DIMS if d != first]
        at = {first: 1 - bit[first], **{d: 1 for d in rest[: k - 2]}, rest[k - 2]: 0}
        return rx0[u].at[tuple(at.get(d, every) for d in DIMS)]

    rx = (rx0, [rx1.at[u] for u in range(UNITS)], *([later(u, k) for u in range(UNITS)] for k in (2, 3, 4)))

    barrier = pltpu.get_barrier_semaphore()
    for d in STRIDE:
        pl.semaphore_signal(barrier, inc=1, device_id=(0, partner[d]), device_id_type=MESH)
    pl.semaphore_wait(barrier, len(STRIDE))

    def fixed(u, k, flip):
        at = {d: bit[d] for d in ORDERS[u][:k]}
        if flip:
            at[ORDERS[u][k - 1]] = 1 - bit[ORDERS[u][k - 1]]
        return at

    def remote(src, dst, send, recv, d):
        return pltpu.make_async_remote_copy(
            src_ref=src, dst_ref=dst, send_sem=send, recv_sem=recv, device_id=(0, partner[d]), device_id_type=MESH
        )

    def scatter(u, k):
        if k == 0:
            src, d = blocks(g_in[place(u)[0]], u, {}, 1 - bit["c"]), "c"
        else:
            at, d = fixed(u, k, True), ORDERS[u][k - 1]
            src = own[u].at[tuple(at.get(d, every) for d in DIMS)]
        return remote(src, rx[k][u], rs_send.at[u, k], rs_recv.at[u, k], d)

    def gather(u, k, receive=False):
        if k == 0:
            return remote(own[u], rx0[u], ag_send.at[u, 0], ag_recv.at[u, 0], "c")
        at = fixed(u, k, receive)
        region = own[u].at[tuple(at.get(d, every) for d in DIMS)]
        return remote(region, region, ag_send.at[u, k], ag_recv.at[u, k], ORDERS[u][k - 1])

    def copy(src, dst, u, i):
        return pltpu.make_async_copy(src, dst, local.at[u, i])

    def load_own(u):
        return copy(blocks(g_in[place(u)[0]], u, {}, bit["c"]), own[u], u, 0)

    def loads(u):
        which = place(u)[0]
        return (
            copy(blocks(w_in[which], u, bit, bit["c"]), w_buf.at[u], u, 1),
            copy(mine(m_in[which], u), m_buf.at[u], u, 2),
            copy(mine(v_in[which], u), v_buf.at[u], u, 3),
        )

    def total(u, at, steps, rows):
        so_far = own[u][(*(at[d] for d in DIMS), rows)].astype(jnp.float32)
        for j in range(steps):
            left = [d for d in DIMS if d not in ORDERS[u][:j]]
            so_far += rx[j][u][(*(at[d] for d in left), rows)].astype(jnp.float32)
        return so_far

    def reduce_to_send(u, k):
        base = fixed(u, k, True)
        free = [d for d in DIMS if d not in base]

        def body(i, carry):
            at = dict(base)
            for p, d in enumerate(reversed(free)):
                at[d] = (i // 2**p) % 2
            for half in range(2):
                rows = pl.ds(half * (ROWS // 2), ROWS // 2)
                own[u][(*(at[d] for d in DIMS), rows)] = total(u, at, k, rows).astype(jnp.bfloat16)
            return carry

        lax.fori_loop(0, 2 ** len(free), body, 0)

    def update(u):
        for half in range(2):
            rows = pl.ds(half * (ROWS // 2), ROWS // 2)
            here = (*(bit[d] for d in DIMS), rows)
            g = total(u, bit, 5, rows).astype(jnp.bfloat16).astype(jnp.float32)
            own[u][here], m_buf[u, rows], v_buf[u, rows] = adamw(w_buf[u, rows].astype(jnp.float32), m_buf[u, rows], v_buf[u, rows], g)

    def release(u, k):
        pl.semaphore_signal(free.at[u, k], inc=1, device_id=(0, partner[ORDERS[u][k - 1] if k else "c"]), device_id_type=MESH)

    def arrived(u, k):
        scatter(u, k).wait_recv()
        if k:
            scatter(u, k).wait_send()
            release(u, k)

    def send_back(u, k):
        pl.semaphore_wait(free.at[u, k], 1)
        gather(u, k).start()

    def event(u, e):
        if e == 0:
            scatter(u, 0).start()
            load_own(u).start()
        elif e <= 4:
            if e == 1:
                load_own(u).wait()
            arrived(u, e - 1)
            reduce_to_send(u, e)
            if e == 1:
                for one in loads(u):
                    one.start()
                for k in (2, 3, 4):
                    pl.semaphore_signal(ready.at[u, k], inc=1, device_id=(0, partner[ORDERS[u][k - 1]]), device_id_type=MESH)
            else:
                pl.semaphore_wait(ready.at[u, e], 1)
            scatter(u, e).start()
        elif e == 5:
            for one in loads(u):
                one.wait()
            arrived(u, 4)
            update(u)
            release(u, 0)
            send_back(u, 4)
        elif e <= 9:
            gather(u, 10 - e, receive=True).wait_recv()
            send_back(u, 9 - e)
        else:
            gather(u, 0, receive=True).wait_recv()

    for code in EVENTS:
        event(*divmod(code, 11))
    for u in range(UNITS):
        scatter(u, 0).wait_send()
        for k in range(5):
            gather(u, k).wait_send()


def write_out(*refs):
    n = UNITS // GROUP
    own, rx0, (m_buf, v_buf) = refs[:n], refs[n : 2 * n], refs[2 * n : 2 * n + 2]
    w_out, m_out, v_out, sems = (*(refs[2 * n + i : 2 * n + i + 3] for i in (2, 5, 8)), refs[2 * n + 11])
    core = lax.axis_index("dp") % 2
    copies = []
    for u in range(UNITS):
        which = place(u)[0]
        for i, (src, dst) in enumerate(
            (
                (own[u // GROUP].at[u % GROUP], blocks(w_out[which], u, {}, core)),
                (rx0[u // GROUP].at[u % GROUP], blocks(w_out[which], u, {}, 1 - core)),
                (m_buf.at[u], mine(m_out[which], u)),
                (v_buf.at[u], mine(v_out[which], u)),
            )
        ):
            copies.append(pltpu.make_async_copy(src, dst, sems.at[u, i]))
    for one in copies:
        one.start()
    for one in copies:
        one.wait()


def solution(mesh):
    def step(*arrays):
        split = [(2, 2, 2, 2, 2, 2, a.shape[-2] // 32, a.shape[-1]) for a in arrays[:3]]
        terms = [a.reshape(s) for a, s in zip(arrays[:3], split)]
        weights = [a.reshape(s) for a, s in zip(arrays[3:6], split)]
        block = (UNITS, ROWS, COLS)
        dma = pltpu.SemaphoreType.DMA
        anywhere = pl.BlockSpec(memory_space=pl.ANY)
        vmem = pl.BlockSpec(memory_space=pltpu.VMEM)
        half = pltpu.VMEM((GROUP, 2, 2, 2, 2, ROWS, COLS), jnp.bfloat16)
        kept = pl.pallas_call(
            kernel,
            out_shape=[half] * (2 * UNITS // GROUP) + [pltpu.VMEM(block, jnp.float32)] * 2,
            in_specs=[anywhere] * 12,
            out_specs=[vmem] * (2 * UNITS // GROUP + 2),
            scratch_shapes=[
                pltpu.VMEM((UNITS, 2, 2, 2, ROWS, COLS), jnp.bfloat16),
                pltpu.VMEM(block, jnp.bfloat16),
                dma((UNITS, 5)),
                dma((UNITS, 5)),
                dma((UNITS, 5)),
                dma((UNITS, 5)),
                dma((UNITS, 4)),
                pltpu.SemaphoreType.REGULAR((UNITS, 5)),
                pltpu.SemaphoreType.REGULAR((UNITS, 5)),
            ],
            compiler_params=pltpu.CompilerParams(collective_id=0, has_side_effects=True, vmem_limit_bytes=KERNEL_VMEM),
            name="zero_step",
        )(*terms, *weights, *(pltpu.with_memory_space_constraint(a, pltpu.HBM) for a in arrays[6:]))
        out = pl.pallas_call(
            write_out,
            out_shape=[jax.ShapeDtypeStruct(s, jnp.bfloat16) for s in split] + [jax.ShapeDtypeStruct(a.shape, a.dtype) for a in arrays[6:]],
            in_specs=[vmem] * (2 * UNITS // GROUP + 2),
            out_specs=[anywhere] * 9,
            scratch_shapes=[dma((UNITS, 4))],
            compiler_params=pltpu.CompilerParams(vmem_limit_bytes=KERNEL_VMEM),
            name="write_out",
        )(*kept)
        return (*(o.reshape(a.shape) for o, a in zip(out[:3], arrays[3:6])), *out[3:])

    all_of, cut = P(None, None, None), P(None, "dp", None)
    return jax.shard_map(
        step,
        mesh=mesh,
        in_specs=(P(("rep", "dp"), None, None, None),) * 3 + (all_of,) * 3 + (cut,) * 6,
        out_specs=(P("rep", None, None),) * 3 + (P("rep", "dp", None),) * 6,
        check_vma=False,
    )
```

time: 296 us -> 288 us (0.973)
  Pallas kernels: 294 us -> 287 us
    pallas_call x1, Pallas kernels: 17.6 us -> 14.2 us  [step(): pl.pallas_call(write_out, out_shape=[jax.ShapeDtypeStruct(s, jnp.bfloat16...]
    pallas_call x1, Pallas kernels: 276 us -> 273 us  [step(): pl.pallas_call(kernel, out_shape=[half] * (2 * UNITS // GROUP) + [pltpu.V...]
where the time goes in v3:
time: 288 us
  Pallas kernels  287 us (100%)
    pallas_call x1, Pallas kernels, step(): pl.pallas_call(kernel, out_shape=[half] * (2 * UNITS // GROUP) + [pltpu.V...  273 us
    pallas_call x1, Pallas kernels, step(): pl.pallas_call(write_out, out_shape=[jax.ShapeDtypeStruct(s, jnp.bfloat16...  14.2 us

profile of v3, /device:TPU:0, one launch (start us, length us, event | category | flops | bytes accessed | tf_op | source)
XLA Modules:
  0.0 287.8 jit_solution(10892244961933457697)
XLA Ops:
  0.6 272.9 %zero_step.1 = (bf16[6,2,2,2,2,32,1024]{6,5,4,3,2,1,0:T(8,128)(2,1)S(1)}, bf16[6,2,2,2,2,32,1024]{6,5,4,3,2,1,0:T(8,128)(2,1)S(1)}, bf16[6,2,2,2,2,32,1024]{6,5,...) custom-call(bf16[2,2,2,2,2,2,32,3072]{7,6,5,4,3,2,1,0:T(8,128)(2,1)}, ...), custom_call_target="tpu_custom_call" | custom-call | tf_op jit(solution)/shard_map/zero_step/pallas_call | solution.py:230
  273.6 14.2 %write_out.1 = (bf16[2,2,2,2,2,2,32,3072]{7,6,5,4,3,2,1,0:T(8,128)(2,1)}, bf16[2,2,2,2,2,2,32,3072]{7,6,5,4,3,2,1,0:T(8,128)(2,1)}, bf16[2,2,2,2,2,2,96,1024]{7,...) custom-call(bf16[6,2,2,2,2,32,1024]{6,5,4,3,2,1,0:T(8,128)(2,1)S(1)}, ...), custom_call_target="tpu_custom_call" | custom-call | tf_op jit(solution)/shard_map/write_out/pallas_call | solution.py:249
